TPU v7x, 32 devices: a whole 2x2x4 slice. The times are simulated.
32 devices in a mesh: tiles: 2 (over x), rows: 8 (over z, y), dates: 2 (over core).
Axes of the slice: x: 2, y: 2, z: 4, core: 2. Of those that a mesh axis runs over, the one named last changes fastest.
Arguments:
- red_band: int32 [24, 512, 2048], P('dates', ('tiles', 'rows')), parts along dimension 1, may hold values from 1 to 1073741823
- nir_band: int32 [24, 512, 2048], P('dates', ('tiles', 'rows')), parts along dimension 1, may hold values from 1 to 1073741823
- cloud_class: int32 [24, 512, 2048], P('dates', ('tiles', 'rows')), parts along dimension 1, may hold values from 0 to 3
- date_ordinal: int32 [48], P(('tiles', 'dates')), parts along dimension 0, may hold values from 0 to 23, each once
Outputs:
- composite_red: int32 [512, 2048], P(('tiles', 'rows', 'dates')), parts along dimension 0
- composite_nir: int32 [512, 2048], P(('tiles', 'rows', 'dates')), parts along dimension 0
- chosen_date: int32 [512, 2048], P(('tiles', 'rows', 'dates')), parts along dimension 0
- overview_one: float32 [2, 256, 1024], P(None, ('tiles', 'rows', 'dates')), parts along dimension 1
- overview_two: float32 [2, 128, 512], P(None, ('tiles', 'rows', 'dates')), parts along dimension 1
- overview_three: float32 [2, 64, 256], P(None, ('tiles', 'rows', 'dates')), parts along dimension 1
There are 2 independent parts, one for each index of `tiles`. A program takes and returns all parts, laid end to end along the dimension named above; each array names one. Nothing has to cross between parts.
Inputs may be any that keep to these rules, and one draw needn't show every extreme that they name: `date_ordinal`: each ordinal appears once.
All inputs are finite; a program needn't handle non-finite values.
Results may differ from a plain program's by a relative error of at most 0.0003.
Values sent between devices are 32-bit elements; how exact they have to be, the bound alone decides.
A program may use at most 192 MiB of HBM per device.

v0:
```python
import jax
import jax.numpy as jnp
from jax import lax
from jax.sharding import PartitionSpec as P

LEVELS = 3


KERNEL = (0.0625, 0.25, 0.375, 0.25, 0.0625)
LIMB = 32768
TWO_LIMBS = 1073741824
SCALE_BAND = 9.313225746154785e-10
FLAG_STEP = 32


def merged_2(value, axis, join):
    pieces = jax.tree.map(lambda part: lax.all_gather(part, axis), value)
    head = jax.tree.map(lambda part: part[0], pieces)
    tail = jax.tree.map(lambda part: part[1:], pieces)
    so_far, _ = lax.scan(lambda so_far, section: (join(so_far, section), None), head, tail)
    return so_far


def padded_2(value, sides, width):
    for axis, dim in sides:
        peers, length = (lax.axis_size(axis), value.shape[dim])
        up = [(i, (i + 1) % peers) for i in range(peers - 1)]
        down = [(j, i) for i, j in up]
        last = lax.slice_in_dim(value, length - width, length, axis=dim)
        first = lax.slice_in_dim(value, 0, width, axis=dim)
        before = lax.ppermute(last, axis, up)
        after = lax.ppermute(first, axis, down)
        value = jnp.concatenate([before, value, after], axis=dim)
    return value


def product_digits(small, large):
    small_hi = small // LIMB
    small_lo = small % LIMB
    large_top = large // TWO_LIMBS
    remain = large % TWO_LIMBS
    large_mid = remain // LIMB
    large_lo = remain % LIMB
    digit_zero = small_lo * large_lo
    digit_one = small_hi * large_lo + small_lo * large_mid
    digit_two = small_hi * large_mid + small_lo * large_top
    digit_three = small_hi * large_top
    digit_one = digit_one + digit_zero // LIMB
    digit_zero = digit_zero % LIMB
    digit_two = digit_two + digit_one // LIMB
    digit_one = digit_one % LIMB
    digit_three = digit_three + digit_two // LIMB
    digit_two = digit_two % LIMB
    return (digit_three, digit_two, digit_one, digit_zero)


def compare_digits(first, second):
    greater = first[0] > second[0]
    equal = first[0] == second[0]
    for one, two in zip(first[1:], second[1:]):
        greater = greater | equal & (one > two)
        equal = equal & (one == two)
    return (greater, equal)


def better(first, second):
    clear_a, red_a, nir_a, ord_a = first
    clear_b, red_b, nir_b, ord_b = second
    diff_a = nir_a - red_a
    diff_b = nir_b - red_b
    total_a = nir_a + red_a
    total_b = nir_b + red_b
    sign_a = jnp.sign(diff_a)
    sign_b = jnp.sign(diff_b)
    greater, equal = compare_digits(
        product_digits(jnp.abs(diff_a), total_b), product_digits(jnp.abs(diff_b), total_a)
    )
    lesser = jnp.logical_not(greater | equal)
    same_sign = sign_a == sign_b
    ndvi_more = (sign_a > sign_b) | same_sign & ((sign_a > 0) & greater | (sign_a < 0) & lesser)
    ndvi_same = same_sign & ((sign_a == 0) | equal)
    same_clear = clear_a == clear_b
    take = (clear_a > clear_b) | same_clear & (ndvi_more | ndvi_same & (ord_a < ord_b))
    return tuple((jnp.where(take, one, two) for one, two in zip(first, second)))


def fold_flag(entries):
    clear, red, nir, ordinal = entries
    return (red, nir, ordinal + FLAG_STEP * clear)


def unfold_flag(packed):
    red, nir, flagged = packed
    clear = (flagged >= FLAG_STEP).astype(jnp.int32)
    return (clear, red, nir, flagged - FLAG_STEP * clear)


def better_packed(first, second):
    return fold_flag(better(unfold_flag(first), unfold_flag(second)))


def smooth_pool(padded, rows):
    cols = padded.shape[2]
    smooth = KERNEL[0] * padded[:, 0:rows]
    for offset in range(1, 5):
        smooth = smooth + KERNEL[offset] * padded[:, offset : offset + rows]
    widened = jnp.pad(smooth, ((0, 0), (0, 0), (2, 2)))
    result = KERNEL[0] * widened[:, :, 0:cols]
    for offset in range(1, 5):
        result = result + KERNEL[offset] * widened[:, :, offset : offset + cols]
    return result.reshape(2, rows // 2, 2, cols // 2, 2).mean(axis=(2, 4))


def body(red_band, nir_band, cloud_class, date_ordinal):
    strip = red_band.shape[1]
    half = strip // 2

    def entry(index):
        return (
            (cloud_class[index] == 0).astype(jnp.int32),
            red_band[index],
            nir_band[index],
            jnp.full(red_band.shape[1:], date_ordinal[index], jnp.int32),
        )

    def advance(carry, index):
        return (better(carry, entry(index)), None)

    best, unused = lax.scan(advance, entry(0), jnp.arange(1, red_band.shape[0], dtype=jnp.int32))
    outgoing = fold_flag(best)
    merged = merged_2(outgoing, "dates", better_packed)
    begin = lax.axis_index("dates") * half
    chosen = tuple((lax.dynamic_slice_in_dim(member, begin, half, 0) for member in merged))
    mine = unfold_flag(chosen)
    level = jnp.stack([mine[1], mine[2]]).astype(jnp.float32) * SCALE_BAND
    levels = []
    for number in range(LEVELS):
        rows = level.shape[1]
        padded = padded_2(level, ((("rows", "dates"), 1),), 2)
        level = smooth_pool(padded, rows)
        levels.append(level)
    return (mine[1], mine[2], mine[3], levels[0], levels[1], levels[2])


def solution(mesh):
    in_specs = (
        P("dates", ("tiles", "rows"), None),
        P("dates", ("tiles", "rows"), None),
        P("dates", ("tiles", "rows"), None),
        P(("tiles", "dates")),
    )
    out_specs = (
        P(("tiles", "rows", "dates"), None),
        P(("tiles", "rows", "dates"), None),
        P(("tiles", "rows", "dates"), None),
        P(None, ("tiles", "rows", "dates"), None),
        P(None, ("tiles", "rows", "dates"), None),
        P(None, ("tiles", "rows", "dates"), None),
    )
    return jax.shard_map(body, mesh=mesh, in_specs=in_specs, out_specs=out_specs, check_vma=False)
```

profile of v0, /device:TPU:1, one launch (start us, length us, event | category | flops | bytes accessed | tf_op | source)
XLA Modules:
  0.0 192.7 jit_solution(100099713657052492)
XLA Ops:
  3.4 113.2 %while.6 = (s32[]{:T(128)}, s32[32,2048]{1,0:T(8,128)S(1)}, s32[32,2048]{1,0:T(8,128)S(1)}, s32[32,2048]{1,0:T(8,128)S(1)}, s32[32,2048]{1,0:T(8,128)S(1)}, /*in...) while((s32[]{:T(128)}, s32[32,2048]{1,0:T(8,128)S(1)}, ...), condition=%wide.region_1.2_spmd, body=%wide.region_0.1_spmd.sunk | while | flops 19857412 | bytes 4456651 | solution.py:129
  5.9 1.2 dynamic_slice.104
  7.2 5.3 %broadcast_select_fusion.2 = (s32[32,2048]{1,0:T(8,128)S(1)}, pred[32,2048]{1,0:T(8,128)(4,1)S(1)}, pred[1,32,2048]{2,1,0:T(8,128)(4,1)S(1)}) fusion(s32[32,2048]{1,0:T(8,128)S(1)} %get-tuple-element.353, s32[]{:T(128)} %bitcast.46, s32[32,2048]{1,0:T(8,128)S(1)} %get-tuple-element.352, s32[32,2048]{1,0:T(8,128)S(1)} %get-tuple-element.351, ...), kind=kLoop, calls=%fused_computation.107.clone.1 | loop fusion | flops 19595264 | bytes 2228232 | tf_op jit(solution)/shard_map/while/body/eval_jaxpr/jit(_where)/select_n | solution.py:84
  16.2 1.2 dynamic_slice.104
  17.5 5.3 %broadcast_select_fusion.2 = (s32[32,2048]{1,0:T(8,128)S(1)}, pred[32,2048]{1,0:T(8,128)(4,1)S(1)}, pred[1,32,2048]{2,1,0:T(8,128)(4,1)S(1)}) fusion(s32[32,2048]{1,0:T(8,128)S(1)} %get-tuple-element.353, s32[]{:T(128)} %bitcast.46, s32[32,2048]{1,0:T(8,128)S(1)} %get-tuple-element.352, s32[32,2048]{1,0:T(8,128)S(1)} %get-tuple-element.351, ...), kind=kLoop, calls=%fused_computation.107.clone.1 | loop fusion | flops 19595264 | bytes 2228232 | tf_op jit(solution)/shard_map/while/body/eval_jaxpr/jit(_where)/select_n | solution.py:84
  27.7 5.3 %broadcast_select_fusion.2 = (s32[32,2048]{1,0:T(8,128)S(1)}, pred[32,2048]{1,0:T(8,128)(4,1)S(1)}, pred[1,32,2048]{2,1,0:T(8,128)(4,1)S(1)}) fusion(s32[32,2048]{1,0:T(8,128)S(1)} %get-tuple-element.353, s32[]{:T(128)} %bitcast.46, s32[32,2048]{1,0:T(8,128)S(1)} %get-tuple-element.352, s32[32,2048]{1,0:T(8,128)S(1)} %get-tuple-element.351, ...), kind=kLoop, calls=%fused_computation.107.clone.1 | loop fusion | flops 19595264 | bytes 2228232 | tf_op jit(solution)/shard_map/while/body/eval_jaxpr/jit(_where)/select_n | solution.py:84
  38.0 5.3 %broadcast_select_fusion.2 = (s32[32,2048]{1,0:T(8,128)S(1)}, pred[32,2048]{1,0:T(8,128)(4,1)S(1)}, pred[1,32,2048]{2,1,0:T(8,128)(4,1)S(1)}) fusion(s32[32,2048]{1,0:T(8,128)S(1)} %get-tuple-element.353, s32[]{:T(128)} %bitcast.46, s32[32,2048]{1,0:T(8,128)S(1)} %get-tuple-element.352, s32[32,2048]{1,0:T(8,128)S(1)} %get-tuple-element.351, ...), kind=kLoop, calls=%fused_computation.107.clone.1 | loop fusion | flops 19595264 | bytes 2228232 | tf_op jit(solution)/shard_map/while/body/eval_jaxpr/jit(_where)/select_n | solution.py:84
  48.3 5.3 %broadcast_select_fusion.2 = (s32[32,2048]{1,0:T(8,128)S(1)}, pred[32,2048]{1,0:T(8,128)(4,1)S(1)}, pred[1,32,2048]{2,1,0:T(8,128)(4,1)S(1)}) fusion(s32[32,2048]{1,0:T(8,128)S(1)} %get-tuple-element.353, s32[]{:T(128)} %bitcast.46, s32[32,2048]{1,0:T(8,128)S(1)} %get-tuple-element.352, s32[32,2048]{1,0:T(8,128)S(1)} %get-tuple-element.351, ...), kind=kLoop, calls=%fused_computation.107.clone.1 | loop fusion | flops 19595264 | bytes 2228232 | tf_op jit(solution)/shard_map/while/body/eval_jaxpr/jit(_where)/select_n | solution.py:84
  58.6 5.3 %broadcast_select_fusion.2 = (s32[32,2048]{1,0:T(8,128)S(1)}, pred[32,2048]{1,0:T(8,128)(4,1)S(1)}, pred[1,32,2048]{2,1,0:T(8,128)(4,1)S(1)}) fusion(s32[32,2048]{1,0:T(8,128)S(1)} %get-tuple-element.353, s32[]{:T(128)} %bitcast.46, s32[32,2048]{1,0:T(8,128)S(1)} %get-tuple-element.352, s32[32,2048]{1,0:T(8,128)S(1)} %get-tuple-element.351, ...), kind=kLoop, calls=%fused_computation.107.clone.1 | loop fusion | flops 19595264 | bytes 2228232 | tf_op jit(solution)/shard_map/while/body/eval_jaxpr/jit(_where)/select_n | solution.py:84
  68.9 5.3 %broadcast_select_fusion.2 = (s32[32,2048]{1,0:T(8,128)S(1)}, pred[32,2048]{1,0:T(8,128)(4,1)S(1)}, pred[1,32,2048]{2,1,0:T(8,128)(4,1)S(1)}) fusion(s32[32,2048]{1,0:T(8,128)S(1)} %get-tuple-element.353, s32[]{:T(128)} %bitcast.46, s32[32,2048]{1,0:T(8,128)S(1)} %get-tuple-element.352, s32[32,2048]{1,0:T(8,128)S(1)} %get-tuple-element.351, ...), kind=kLoop, calls=%fused_computation.107.clone.1 | loop fusion | flops 19595264 | bytes 2228232 | tf_op jit(solution)/shard_map/while/body/eval_jaxpr/jit(_where)/select_n | solution.py:84
  79.2 5.3 %broadcast_select_fusion.2 = (s32[32,2048]{1,0:T(8,128)S(1)}, pred[32,2048]{1,0:T(8,128)(4,1)S(1)}, pred[1,32,2048]{2,1,0:T(8,128)(4,1)S(1)}) fusion(s32[32,2048]{1,0:T(8,128)S(1)} %get-tuple-element.353, s32[]{:T(128)} %bitcast.46, s32[32,2048]{1,0:T(8,128)S(1)} %get-tuple-element.352, s32[32,2048]{1,0:T(8,128)S(1)} %get-tuple-element.351, ...), kind=kLoop, calls=%fused_computation.107.clone.1 | loop fusion | flops 19595264 | bytes 2228232 | tf_op jit(solution)/shard_map/while/body/eval_jaxpr/jit(_where)/select_n | solution.py:84
  89.5 5.3 %broadcast_select_fusion.2 = (s32[32,2048]{1,0:T(8,128)S(1)}, pred[32,2048]{1,0:T(8,128)(4,1)S(1)}, pred[1,32,2048]{2,1,0:T(8,128)(4,1)S(1)}) fusion(s32[32,2048]{1,0:T(8,128)S(1)} %get-tuple-element.353, s32[]{:T(128)} %bitcast.46, s32[32,2048]{1,0:T(8,128)S(1)} %get-tuple-element.352, s32[32,2048]{1,0:T(8,128)S(1)} %get-tuple-element.351, ...), kind=kLoop, calls=%fused_computation.107.clone.1 | loop fusion | flops 19595264 | bytes 2228232 | tf_op jit(solution)/shard_map/while/body/eval_jaxpr/jit(_where)/select_n | solution.py:84
  99.8 5.3 %broadcast_select_fusion.2 = (s32[32,2048]{1,0:T(8,128)S(1)}, pred[32,2048]{1,0:T(8,128)(4,1)S(1)}, pred[1,32,2048]{2,1,0:T(8,128)(4,1)S(1)}) fusion(s32[32,2048]{1,0:T(8,128)S(1)} %get-tuple-element.353, s32[]{:T(128)} %bitcast.46, s32[32,2048]{1,0:T(8,128)S(1)} %get-tuple-element.352, s32[32,2048]{1,0:T(8,128)S(1)} %get-tuple-element.351, ...), kind=kLoop, calls=%fused_computation.107.clone.1 | loop fusion | flops 19595264 | bytes 2228232 | tf_op jit(solution)/shard_map/while/body/eval_jaxpr/jit(_where)/select_n | solution.py:84
  110.0 5.3 %broadcast_select_fusion.2 = (s32[32,2048]{1,0:T(8,128)S(1)}, pred[32,2048]{1,0:T(8,128)(4,1)S(1)}, pred[1,32,2048]{2,1,0:T(8,128)(4,1)S(1)}) fusion(s32[32,2048]{1,0:T(8,128)S(1)} %get-tuple-element.353, s32[]{:T(128)} %bitcast.46, s32[32,2048]{1,0:T(8,128)S(1)} %get-tuple-element.352, s32[32,2048]{1,0:T(8,128)S(1)} %get-tuple-element.351, ...), kind=kLoop, calls=%fused_computation.107.clone.1 | loop fusion | flops 19595264 | bytes 2228232 | tf_op jit(solution)/shard_map/while/body/eval_jaxpr/jit(_where)/select_n | solution.py:84
  116.6 2.2 %all-gather = s32[64,2048]{1,0:T(8,128)S(1)} all-gather(s32[32,2048]{1,0:T(8,128)S(1)} %multiply_add_fusion.1), channel_id=2, replica_groups=mesh['tiles'=2,'rows'=8,'dates'=2] {'dates'}, dimensions={0}, use_global_device_ids=true | all-gather | bytes 786432 | tf_op jit(solution)/shard_map/all_gather | solution.py:17
  118.8 2.2 %all-gather.2 = s32[64,2048]{1,0:T(8,128)S(1)} all-gather(s32[32,2048]{1,0:T(8,128)S(1)} %get-tuple-element.212), channel_id=4, replica_groups=mesh['tiles'=2,'rows'=8,'dates'=2] {'dates'}, dimensions={0}, use_global_device_ids=true | all-gather | bytes 786432 | tf_op jit(solution)/shard_map/all_gather | solution.py:17
  120.9 2.2 %all-gather.1 = s32[64,2048]{1,0:T(8,128)S(1)} all-gather(s32[32,2048]{1,0:T(8,128)S(1)} %get-tuple-element.211), channel_id=3, replica_groups=mesh['tiles'=2,'rows'=8,'dates'=2] {'dates'}, dimensions={0}, use_global_device_ids=true | all-gather | bytes 786432 | tf_op jit(solution)/shard_map/all_gather | solution.py:17
  124.0 3.5 %fusion.105 = (s32[32,2048]{1,0:T(8,128)S(1)}, pred[32,2048]{1,0:T(8,128)(4,1)S(1)}, s32[32,2048]{1,0:T(8,128)S(1)}) fusion(pred[32,2048]{1,0:T(8,128)(4,1)S(1)} %get-tuple-element.237, pred[32,2048]{1,0:T(8,128)(4,1)S(1)} %get-tuple-element.246, s32[64,2048]{1,0:T(8,128)S(1)} %all-gather, s32[64,2048]{1,0:T(8,128)S(1)} %all-gather.2, ...), kind=kLoop, calls=%fused_computation.307 | loop fusion | flops 19791872 | bytes 2293760 | tf_op jit(solution)/shard_map/while/body/eval_jaxpr/convert_element_type | solution.py:94
  127.5 1.6 select_subtract_fusion.2
  129.2 4.5 %collective-permute-start = (f32[2,2,2048]{2,1,0:T(2,128)S(1)}, f32[2,2,2048]{2,1,0:T(2,128)S(1)}, u32[]{:S(2)}, u32[]{:S(2)}) collective-permute-start(f32[2,2,2048]{2,1,0:T(2,128)S(1)} %get-tuple-element.249), channel_id=1, source_target_pairs={{0,1},{1,2},{2,3},{3,4},{4,5},{5,6},{6,7},{7,8},{8,9},{9,10},{10,1... | collective-permute-start | bytes 98312 | tf_op jit(solution)/shard_map/ppermute | solution.py:31
  133.8 2.1 %collective-permute-start.1 = (f32[2,2,2048]{2,1,0:T(2,128)S(1)}, f32[2,2,2048]{2,1,0:T(2,128)S(1)}, u32[]{:S(2)}, u32[]{:S(2)}) collective-permute-start(f32[2,2,2048]{2,1,0:T(2,128)S(1)} %get-tuple-element.250), channel_id=1, source_target_pairs={{1,0},{2,1},{3,2},{4,3},{5,4},{6,5},{7,6},{8,7},{9,8},{10,9},{11,1... | collective-permute-start | bytes 98312 | tf_op jit(solution)/shard_map/ppermute | solution.py:32
  135.9 3.1 %collective-permute-done.1 = f32[2,2,2048]{2,1,0:T(2,128)S(1)} collective-permute-done((f32[2,2,2048]{2,1,0:T(2,128)S(1)}, f32[2,2,2048]{2,1,0:T(2,128)S(1)}, u32[]{:S(2)}, u32[]{:S(2)}) %collective-permute-start.1) | collective-permute-done | bytes 32800 | tf_op jit(solution)/shard_map/ppermute | solution.py:32
  139.5 19.0 %reshape.29 = f32[2,8,2,1024,2]{4,3,2,1,0:T(8,128)} reshape(f32[2,16,2048]{2,1,0:T(8,128)S(1)} %multiply_add_fusion) | data formatting | bytes 524288 | tf_op jit(solution)/shard_map/reshape | solution.py:111
  158.5 8.0 %reduce_sum.27 = f32[2,8,1024]{2,1,0:T(8,128)S(1)} reduce(f32[2,8,2,1024,2]{4,3,2,1,0:T(8,128)} %reshape.29, f32[]{:T(128)} %constant.498.clone.1), dimensions={2,4}, to_apply=%region_2.3 | reduce | flops 49152 | bytes 327684 | tf_op jit(solution)/shard_map/reduce_sum | solution.py:111
  166.6 1.9 collective-permute-start.2
  168.5 2.4 %collective-permute-start.3 = (f32[2,2,1024]{2,1,0:T(2,128)S(1)}, f32[2,2,1024]{2,1,0:T(2,128)S(1)}, u32[]{:S(2)}, u32[]{:S(2)}) collective-permute-start(f32[2,2,1024]{2,1,0:T(2,128)S(1)} %get-tuple-element.252), channel_id=1, source_target_pairs={{1,0},{2,1},{3,2},{4,3},{5,4},{6,5},{7,6},{8,7},{9,8},{10,9},{11,1... | collective-permute-start | bytes 49160 | tf_op jit(solution)/shard_map/ppermute | solution.py:32
  170.9 3.4 %collective-permute-done.3 = f32[2,2,1024]{2,1,0:T(2,128)S(1)} collective-permute-done((f32[2,2,1024]{2,1,0:T(2,128)S(1)}, f32[2,2,1024]{2,1,0:T(2,128)S(1)}, u32[]{:S(2)}, u32[]{:S(2)}) %collective-permute-start.3) | collective-permute-done | bytes 16416 | tf_op jit(solution)/shard_map/ppermute | solution.py:32
  174.6 5.5 %reshape.30 = f32[2,4,2,512,2]{4,3,2,1,0:T(8,128)} reshape(f32[2,8,1024]{2,1,0:T(8,128)S(1)} %fusion.68) | data formatting | bytes 131072 | tf_op jit(solution)/shard_map/reshape | solution.py:111
  180.1 2.8 %reduce_sum.28 = f32[2,4,512]{2,1,0:T(4,128)S(1)} reduce(f32[2,4,2,512,2]{4,3,2,1,0:T(8,128)} %reshape.30, f32[]{:T(128)} %constant.498.clone.1), dimensions={2,4}, to_apply=%region_3.4 | reduce | flops 12288 | bytes 81924 | tf_op jit(solution)/shard_map/reduce_sum | solution.py:111
  183.0 1.9 %collective-permute-start.4 = (f32[2,2,512]{2,1,0:T(2,128)S(1)}, f32[2,2,512]{2,1,0:T(2,128)S(1)}, u32[]{:S(2)}, u32[]{:S(2)}) collective-permute-start(f32[2,2,512]{2,1,0:T(2,128)S(1)} %get-tuple-element.259), channel_id=1, source_target_pairs={{0,1},{1,2},{2,3},{3,4},{4,5},{5,6},{6,7},{7,8},{8,9},{9,10},{10,1... | collective-permute-start | bytes 24584 | tf_op jit(solution)/shard_map/ppermute | solution.py:31
  184.9 2.4 %collective-permute-start.5 = (f32[2,2,512]{2,1,0:T(2,128)S(1)}, f32[2,2,512]{2,1,0:T(2,128)S(1)}, u32[]{:S(2)}, u32[]{:S(2)}) collective-permute-start(f32[2,2,512]{2,1,0:T(2,128)S(1)} %get-tuple-element.260), channel_id=1, source_target_pairs={{1,0},{2,1},{3,2},{4,3},{5,4},{6,5},{7,6},{8,7},{9,8},{10,9},{11,1... | collective-permute-start | bytes 24584 | tf_op jit(solution)/shard_map/ppermute | solution.py:32
  187.3 3.4 %collective-permute-done.5 = f32[2,2,512]{2,1,0:T(2,128)S(1)} collective-permute-done((f32[2,2,512]{2,1,0:T(2,128)S(1)}, f32[2,2,512]{2,1,0:T(2,128)S(1)}, u32[]{:S(2)}, u32[]{:S(2)}) %collective-permute-start.5) | collective-permute-done | bytes 8224 | tf_op jit(solution)/shard_map/ppermute | solution.py:32
  (65 shorter events, 37.6 us)
Async XLA Ops:
  129.2 29.4 %copy-start = (s32[16,2048]{1,0:T(8,128)}, s32[16,2048]{1,0:T(8,128)S(1)}, u32[]{:S(2)}) copy-start(s32[16,2048]{1,0:T(8,128)S(1)} %get-tuple-element.254) | copy-start | bytes 393220
  129.2 29.4 %copy-start.1 = (s32[16,2048]{1,0:T(8,128)}, s32[16,2048]{1,0:T(8,128)S(1)}, u32[]{:S(2)}) copy-start(s32[16,2048]{1,0:T(8,128)S(1)} %get-tuple-element.255) | copy-start | bytes 393220
  129.2 6.6 %collective-permute-start = (f32[2,2,2048]{2,1,0:T(2,128)S(1)}, f32[2,2,2048]{2,1,0:T(2,128)S(1)}, u32[]{:S(2)}, u32[]{:S(2)}) collective-permute-start(f32[2,2,2048]{2,1,0:T(2,128)S(1)} %get-tuple-element.249), channel_id=1, source_target_pairs={{0,1},{1,2},{2,3},{3,4},{4,5},{5,6},{6,7},{7,8},{8,9},{9,10},{10,1... | collective-permute-start | bytes 98312 | tf_op jit(solution)/shard_map/ppermute | solution.py:31
  133.8 5.2 %collective-permute-start.1 = (f32[2,2,2048]{2,1,0:T(2,128)S(1)}, f32[2,2,2048]{2,1,0:T(2,128)S(1)}, u32[]{:S(2)}, u32[]{:S(2)}) collective-permute-start(f32[2,2,2048]{2,1,0:T(2,128)S(1)} %get-tuple-element.250), channel_id=1, source_target_pairs={{1,0},{2,1},{3,2},{4,3},{5,4},{6,5},{7,6},{8,7},{9,8},{10,9},{11,1... | collective-permute-start | bytes 98312 | tf_op jit(solution)/shard_map/ppermute | solution.py:32
  166.6 16.3 %copy-start.2 = (f32[2,8,1024]{2,1,0:T(8,128)}, f32[2,8,1024]{2,1,0:T(8,128)S(1)}, u32[]{:S(2)}) copy-start(f32[2,8,1024]{2,1,0:T(8,128)S(1)} %broadcast_multiply_fusion) | copy-start | bytes 196612
  166.6 4.3 %collective-permute-start.2 = (f32[2,2,1024]{2,1,0:T(2,128)S(1)}, f32[2,2,1024]{2,1,0:T(2,128)S(1)}, u32[]{:S(2)}, u32[]{:S(2)}) collective-permute-start(f32[2,2,1024]{2,1,0:T(2,128)S(1)} %get-tuple-element.251), channel_id=1, source_target_pairs={{0,1},{1,2},{2,3},{3,4},{4,5},{5,6},{6,7},{7,8},{8,9},{9,10},{10,1... | collective-permute-start | bytes 49160 | tf_op jit(solution)/shard_map/ppermute | solution.py:31
  168.5 5.8 %collective-permute-start.3 = (f32[2,2,1024]{2,1,0:T(2,128)S(1)}, f32[2,2,1024]{2,1,0:T(2,128)S(1)}, u32[]{:S(2)}, u32[]{:S(2)}) collective-permute-start(f32[2,2,1024]{2,1,0:T(2,128)S(1)} %get-tuple-element.252), channel_id=1, source_target_pairs={{1,0},{2,1},{3,2},{4,3},{5,4},{6,5},{7,6},{8,7},{9,8},{10,9},{11,1... | collective-permute-start | bytes 49160 | tf_op jit(solution)/shard_map/ppermute | solution.py:32
  182.9 9.8 %copy-start.3 = (f32[2,4,512]{2,1,0:T(4,128)}, f32[2,4,512]{2,1,0:T(4,128)S(1)}, u32[]{:S(2)}) copy-start(f32[2,4,512]{2,1,0:T(4,128)S(1)} %broadcast_multiply_fusion.1) | copy-start | bytes 49156
  183.0 4.3 %collective-permute-start.4 = (f32[2,2,512]{2,1,0:T(2,128)S(1)}, f32[2,2,512]{2,1,0:T(2,128)S(1)}, u32[]{:S(2)}, u32[]{:S(2)}) collective-permute-start(f32[2,2,512]{2,1,0:T(2,128)S(1)} %get-tuple-element.259), channel_id=1, source_target_pairs={{0,1},{1,2},{2,3},{3,4},{4,5},{5,6},{6,7},{7,8},{8,9},{9,10},{10,1... | collective-permute-start | bytes 24584 | tf_op jit(solution)/shard_map/ppermute | solution.py:31
  184.9 5.9 %collective-permute-start.5 = (f32[2,2,512]{2,1,0:T(2,128)S(1)}, f32[2,2,512]{2,1,0:T(2,128)S(1)}, u32[]{:S(2)}, u32[]{:S(2)}) collective-permute-start(f32[2,2,512]{2,1,0:T(2,128)S(1)} %get-tuple-element.260), channel_id=1, source_target_pairs={{1,0},{2,1},{3,2},{4,3},{5,4},{6,5},{7,6},{8,7},{9,8},{10,9},{11,1... | collective-permute-start | bytes 24584 | tf_op jit(solution)/shard_map/ppermute | solution.py:32
where the time goes:
time: 194 us; the launch traced here: 193 us
  other arithmetic  91 us (47%)
  local copies, waits for them, and re-layouts  47.5 us (24%)
  loops' own time  21.6 us (11%)
  starting transfers between devices  15.3 us (8%)
  waiting for transfers between devices  10 us (5%)
  blocking collectives  6.52 us (3%)
    select_n x22, other arithmetic, better(): return tuple((jnp.where(take, one, two) for one, two in zip(first, second)))  71.4 us
    reshape x3, local copies, waits for them, and re-layouts, smooth_pool(): return result.reshape(2, rows // 2, 2, cols // 2, 2).mean(axis=(2, 4))  25.5 us
    another operation x1, loops' own time, body(): lax.scan(advance, entry(0), jnp.arange(1, red_band.shape[0], dtype=jnp.in...  21.6 us
    dynamic_slice x11, local copies, waits for them, and re-layouts, entry(): date_ordinal[index]  13.7 us
    reduce_sum x3, other arithmetic, smooth_pool(): return result.reshape(2, rows // 2, 2, cols // 2, 2).mean(axis=(2, 4))  11 us
    ppermute x3, waiting for transfers between devices, padded_2(): after = lax.ppermute(first, axis, down)  9.99 us
    ppermute x3, starting transfers between devices, padded_2(): before = lax.ppermute(last, axis, up)  8.38 us
    ppermute x3, starting transfers between devices, padded_2(): after = lax.ppermute(first, axis, down)  6.89 us
  transfers between devices with their start and end apart: 6, of which 3 were waited for; matrix products, arithmetic and copies ran while one was open for 0% of the time, Pallas kernels for 0%

commit v1 on v0

v1 whole, which is shorter than its diff:
```python
import functools

import jax
import jax.numpy as jnp
from jax import lax
from jax.experimental import pallas as pl
from jax.experimental.pallas import tpu as pltpu
from jax.sharding import PartitionSpec as P

LEVELS = 3
LIMB_BITS = 15
LIMB_MASK = (1 << LIMB_BITS) - 1
FLAG = 1 << 30
SCALE_BAND = 2.0**-30
LANES = 128
WIDTH = 256
MESH = pl.DeviceIdType.MESH


def taps(distance):
    far = (distance == 0) | (distance == 5)
    mid = (distance == 1) | (distance == 4)
    near = (distance == 2) | (distance == 3)
    return jnp.where(near, 0.3125, jnp.where(mid, 0.15625, jnp.where(far, 0.03125, 0.0)))


def limbs(value):
    return value >> LIMB_BITS, value & LIMB_MASK


def take_first(first, second):
    r1a, r0a, n1a, n0a, clear_a, ord_a = first
    r1b, r0b, n1b, n0b, clear_b, ord_b = second
    low = n0a * r0b - n0b * r0a + ((ord_b - ord_a) >> 31)
    mid = (n1a * r0b + n0a * r1b) - (n1b * r0a + n0b * r1a) + (low >> LIMB_BITS)
    high = n1a * r1b - n1b * r1a + (mid >> LIMB_BITS)
    return high + (clear_a - clear_b) >= 0


def pick(take, first, second):
    return tuple(jnp.where(take, one, two) for one, two in zip(first, second))


def joined(entry):
    r1, r0, n1, n0, clear, order = entry
    return (r1 << LIMB_BITS) | r0, (n1 << LIMB_BITS) | n0, clear, order


def dot_split(left, right, exact_left):
    data = right if exact_left else left
    high = data.astype(jnp.bfloat16)
    low = (data - high.astype(jnp.float32)).astype(jnp.bfloat16)
    if exact_left:
        dot = lambda part: jnp.dot(left, part, preferred_element_type=jnp.float32)
    else:
        dot = lambda part: jnp.dot(part, right, preferred_element_type=jnp.float32)
    return dot(high) + dot(low)


def filter_columns(source, weights):
    rows = source.shape[0]
    blocks = (source.shape[1] - 2 * LANES) // (2 * LANES)
    left = jnp.concatenate([source[:, 2 * LANES * b : 2 * LANES * b + 4 * LANES] for b in range(blocks)], axis=0)
    out = dot_split(left, weights, False)
    return [out[b * rows : (b + 1) * rows] for b in range(blocks)]


def iota(shape, axis):
    return lax.broadcasted_iota(jnp.int32, shape, axis)


def kernel(
    red, nir, cloud, ords, out_red, out_nir, out_ord, out_1, out_2, out_3,
    in_red, in_nir, in_cloud, best, arrived, wide_0, ybuf, wide_1, wide_2, zbuf,
    load_sem, send_sem, recv_sem,
):
    tile = lax.axis_index("tiles")
    strip_index = lax.axis_index("rows")
    core = lax.axis_index("dates")
    strips = lax.axis_size("rows")
    dates, strip, width = red.shape
    chunk = strip // 4
    half = width // 2
    has_outer = jnp.where(core == 0, strip_index > 0, strip_index < strips - 1)
    outer_strip = jnp.clip(strip_index + 2 * core - 1, 0, strips - 1)
    partner = (tile, strip_index, 1 - core)
    outer = (tile, outer_strip, 1 - core)
    rows_of = [(3 - 3 * core) * chunk, 3 * core * chunk, (2 - core) * chunk, (1 + core) * chunk]

    loads = []
    for slot, begin in enumerate(rows_of):
        begin = pl.multiple_of(begin, chunk)
        group = [
            pltpu.make_async_copy(
                source.at[:, pl.ds(begin, chunk), :], target.at[slot], load_sem.at[slot, number]
            )
            for number, (source, target) in enumerate(((red, in_red), (nir, in_nir), (cloud, in_cloud)))
        ]
        for copy in group:
            copy.start()
        loads.append(group)

    barrier = pltpu.get_barrier_semaphore()
    pl.semaphore_signal(barrier, inc=1, device_id=partner, device_id_type=MESH)

    @pl.when(has_outer)
    def _():
        pl.semaphore_signal(barrier, inc=1, device_id=outer, device_id_type=MESH)

    k = iota((4 * LANES, LANES), 0)
    j = iota((4 * LANES, LANES), 1)
    column_weights = taps(k - LANES - (2 * j - 2)).astype(jnp.bfloat16)

    @pl.when(jnp.logical_not(has_outer))
    def _():
        ybuf[3] = jnp.zeros(ybuf.shape[1:], jnp.float32)
        zbuf[2] = jnp.zeros(zbuf.shape[1:], jnp.float32)

    for wide in (wide_0, wide_1, wide_2):
        edge = jnp.zeros((wide.shape[0], LANES), jnp.float32)
        wide[:, 0:LANES] = edge
        wide[:, wide.shape[1] - LANES :] = edge

    def find_best(slot):
        for copy in loads[slot]:
            copy.wait()

        def step(number, unused):
            columns = pl.ds(pl.multiple_of(number * WIDTH, WIDTH), WIDTH)

            def entry(date):
                red_hi, red_lo = limbs(in_red[slot, date, :, columns])
                nir_hi, nir_lo = limbs(in_nir[slot, date, :, columns])
                clear = jnp.where(in_cloud[slot, date, :, columns] == 0, FLAG, 0)
                return (red_hi, red_lo, nir_hi, nir_lo, clear, jnp.full((chunk, WIDTH), ords[date], jnp.int32))

            current = entry(0)
            for date in range(1, dates):
                other = entry(date)
                current = pick(take_first(other, current), other, current)
            value_red, value_nir, clear, order = joined(current)
            best[slot, 0, :, columns] = value_red
            best[slot, 1, :, columns] = value_nir
            best[slot, 2, :, columns] = clear + order
            return unused

        lax.fori_loop(0, width // WIDTH, step, 0)

    def send_best(slot, place):
        copy = pltpu.make_async_remote_copy(
            src_ref=best.at[slot],
            dst_ref=arrived.at[place],
            send_sem=send_sem.at[place],
            recv_sem=recv_sem.at[place],
            device_id=partner,
            device_id_type=MESH,
        )
        copy.start()
        return copy

    def merge(slot, place, out_row):
        def step(number, unused):
            at = pl.multiple_of(number * WIDTH, WIDTH)
            columns = pl.ds(at, WIDTH)

            def entry(source):
                red_hi, red_lo = limbs(source[0, :, columns])
                nir_hi, nir_lo = limbs(source[1, :, columns])
                packed = source[2, :, columns]
                return (red_hi, red_lo, nir_hi, nir_lo, packed & FLAG, packed & (FLAG - 1))

            mine, theirs = entry(best.at[slot]), entry(arrived.at[place])
            value_red, value_nir, clear, order = joined(pick(take_first(theirs, mine), theirs, mine))
            if out_row is not None:
                rows = pl.ds(pl.multiple_of(out_row, chunk), chunk)
                out_red[rows, columns] = value_red
                out_nir[rows, columns] = value_nir
                out_ord[rows, columns] = order
            inner = pl.ds(pl.multiple_of(at + LANES, LANES), WIDTH)
            wide_0[0:chunk, inner] = value_red.astype(jnp.float32) * SCALE_BAND
            wide_0[chunk : 2 * chunk, inner] = value_nir.astype(jnp.float32) * SCALE_BAND
            return unused

        lax.fori_loop(0, width // WIDTH, step, 0)

    def columns_of(place):
        for number, block in enumerate(filter_columns(wide_0, column_weights)):
            ybuf[place, :, number * LANES : (number + 1) * LANES] = block

    find_best(0)
    pl.semaphore_wait(barrier, 1 + has_outer.astype(jnp.int32))
    send_0 = send_best(0, 0)
    find_best(1)
    send_0.wait_recv()
    merge(1, 0, core * chunk)
    columns_of(0)
    halo = pltpu.make_async_remote_copy(
        src_ref=ybuf.at[0],
        dst_ref=ybuf.at[3],
        send_sem=send_sem.at[3],
        recv_sem=recv_sem.at[3],
        device_id=outer,
        device_id_type=MESH,
    )

    @pl.when(has_outer)
    def _():
        halo.start()

    find_best(2)
    send_1 = send_best(2, 1)
    find_best(3)
    send_2 = send_best(3, 2)
    send_1.wait_recv()
    merge(3, 1, (1 - core) * chunk)
    columns_of(1)

    quarter = chunk // 2
    m = iota((4 * chunk, 8 * chunk), 0)
    band_m = m // (2 * chunk)
    within = m % (2 * chunk)
    row_1 = jnp.where(within < chunk, within, jnp.where(within < chunk + quarter, within - chunk - quarter, within - quarter))
    c = iota((4 * chunk, 8 * chunk), 1)
    place = c // (2 * chunk)
    band_c = (c // chunk) % 2
    from_core_0 = jnp.where(place == 3, -chunk, place * chunk)
    from_core_1 = chunk - from_core_0
    row_0 = jnp.where(core == 0, from_core_0, from_core_1) + c % chunk
    from_edge = jnp.where(core == 0, row_1, chunk - 1 - row_1)
    inside = from_edge >= jnp.where(has_outer, -chunk, 0)
    rows_1 = jnp.where((band_m == band_c) & inside, taps(row_0 - (2 * row_1 - 2)), 0.0)
    rows_1 = rows_1.astype(jnp.bfloat16)

    m = iota((3 * chunk, 4 * chunk), 0)
    packed = m >= 2 * chunk
    band_m = jnp.where(packed, (m - 2 * chunk) // quarter, m // chunk)
    row_2 = jnp.where(packed, m % quarter, m % chunk)
    c = iota((3 * chunk, 4 * chunk), 1)
    band_c = c // (2 * chunk)
    within = c % (2 * chunk)
    row_1 = jnp.where(within < chunk, within, jnp.where(within < chunk + quarter, within - chunk - quarter, within - quarter))
    rows_2 = jnp.where(band_m == band_c, taps(row_1 - (2 * row_2 - 2)), 0.0).astype(jnp.bfloat16)

    m = iota((2 * chunk, 3 * chunk), 0)
    c = iota((2 * chunk, 3 * chunk), 1)
    place = c // chunk
    toward = quarter * (1 - 2 * core)
    side = jnp.where(place == 0, 0, jnp.where(place == 1, toward, -toward))
    row_2 = c % quarter + side
    rows_3 = jnp.where(m // chunk == (c % chunk) // quarter, taps(row_2 - (2 * (m % chunk) - 2)), 0.0)
    rows_3 = rows_3.astype(jnp.bfloat16)

    send_2.wait_recv()
    merge(2, 2, None)
    columns_of(2)

    @pl.when(has_outer)
    def _():
        halo.wait_recv()

    level_1 = dot_split(rows_1, ybuf[...].reshape(8 * chunk, half), True)
    wide_1[:, LANES : LANES + half] = level_1
    out_1[0] = level_1[0:chunk]
    out_1[1] = level_1[2 * chunk : 3 * chunk]
    data = jnp.concatenate(filter_columns(wide_1, column_weights), axis=1)
    level_2 = dot_split(rows_2, data, True)
    wide_2[:, LANES : LANES + half // 2] = level_2[2 * chunk :]
    out_2[0] = level_2[0:quarter]
    out_2[1] = level_2[chunk : chunk + quarter]
    zbuf[0] = jnp.concatenate(filter_columns(wide_2, column_weights), axis=1)

    def send_z(slot, device):
        return pltpu.make_async_remote_copy(
            src_ref=zbuf.at[0],
            dst_ref=zbuf.at[slot],
            send_sem=send_sem.at[3 + slot],
            recv_sem=recv_sem.at[3 + slot],
            device_id=device,
            device_id_type=MESH,
        )

    to_partner, to_outer = send_z(1, partner), send_z(2, outer)

    @pl.when(has_outer)
    def _():
        to_outer.start()

    to_partner.start()
    to_partner.wait_recv()

    @pl.when(has_outer)
    def _():
        to_outer.wait_recv()

    level_3 = dot_split(rows_3, zbuf[...].reshape(3 * chunk, zbuf.shape[2]), True)
    out_3[0] = level_3[0 : quarter // 2]
    out_3[1] = level_3[chunk : chunk + quarter // 2]

    for copy in (send_0, send_1, send_2, to_partner):
        copy.wait_send()

    @pl.when(has_outer)
    def _():
        halo.wait_send()
        to_outer.wait_send()


def body(red_band, nir_band, cloud_class, date_ordinal):
    dates, strip, width = red_band.shape
    own = strip // 2
    chunk = strip // 4
    whole = pl.BlockSpec(memory_space=pltpu.VMEM)
    anywhere = pl.BlockSpec(memory_space=pl.ANY)
    outs = [jax.ShapeDtypeStruct((own, width), jnp.int32)] * 3
    outs += [jax.ShapeDtypeStruct((2, own >> n, width >> n), jnp.float32) for n in range(1, LEVELS + 1)]
    stream = pltpu.VMEM((4, dates, chunk, width), jnp.int32)
    return pl.pallas_call(
        kernel,
        out_shape=outs,
        in_specs=[anywhere] * 3 + [pl.BlockSpec(memory_space=pltpu.SMEM)],
        out_specs=[whole] * 6,
        scratch_shapes=[
            stream,
            stream,
            stream,
            pltpu.VMEM((4, 3, chunk, width), jnp.int32),
            pltpu.VMEM((3, 3, chunk, width), jnp.int32),
            pltpu.VMEM((2 * chunk, width + 2 * LANES), jnp.float32),
            pltpu.VMEM((4, 2 * chunk, width // 2), jnp.float32),
            pltpu.VMEM((4 * chunk, width // 2 + 2 * LANES), jnp.float32),
            pltpu.VMEM((chunk, width // 4 + 2 * LANES), jnp.float32),
            pltpu.VMEM((3, chunk, width // 8), jnp.float32),
            pltpu.SemaphoreType.DMA((4, 3)),
            pltpu.SemaphoreType.DMA((6,)),
            pltpu.SemaphoreType.DMA((6,)),
        ],
        compiler_params=pltpu.CompilerParams(collective_id=0, has_side_effects=True),
        name="composite",
    )(red_band, nir_band, cloud_class, date_ordinal)


def solution(mesh):
    in_specs = (
        P("dates", ("tiles", "rows"), None),
        P("dates", ("tiles", "rows"), None),
        P("dates", ("tiles", "rows"), None),
        P(("tiles", "dates")),
    )
    out_specs = (
        P(("tiles", "rows", "dates"), None),
        P(("tiles", "rows", "dates"), None),
        P(("tiles", "rows", "dates"), None),
        P(None, ("tiles", "rows", "dates"), None),
        P(None, ("tiles", "rows", "dates"), None),
        P(None, ("tiles", "rows", "dates"), None),
    )
    return jax.shard_map(body, mesh=mesh, in_specs=in_specs, out_specs=out_specs, check_vma=False)
```

time: 194 us -> 24.5 us (0.13)
  other arithmetic: 91 us -> 0 us
  local copies, waits for them, and re-layouts: 47.5 us -> 8.77 us
  loops' own time: 21.6 us -> 0 us
  starting transfers between devices: 15.3 us -> 0 us
  Pallas kernels: 0 us -> 14.7 us
  waiting for transfers between devices: 10 us -> 0 us
  blocking collectives: 6.52 us -> 0 us
    select_n x22 -> x0, other arithmetic: 71.4 us -> none  [better(): return tuple((jnp.where(take, one, two) for one, two in zip(first, second)))]
    reshape x3 -> x0, local copies, waits for them, and re-layouts: 25.5 us -> none  [smooth_pool(): return result.reshape(2, rows // 2, 2, cols // 2, 2).mean(axis=(2, 4))]
    another operation x1 -> x0, loops' own time: 21.6 us -> none  [body(): lax.scan(advance, entry(0), jnp.arange(1, red_band.shape[0], dtype=jnp.in...]
    dynamic_slice x22 -> x0, local copies, waits for them, and re-layouts: 20.1 us -> none  [the longest x11 13.7 us: entry(): date_ordinal[index]]
    ppermute x6 -> x0, starting transfers between devices: 15.3 us -> none  [the longest x3 8.38 us: padded_2(): before = lax.ppermute(last, axis, up)]
    pallas_call x0 -> x1, Pallas kernels: none -> 14.7 us  [body(): pl.pallas_call(kernel, out_shape=outs, in_specs=[anywhere] * 3 + [pl.Bloc...]
    reduce_sum x3 -> x0, other arithmetic: 11 us -> none  [smooth_pool(): return result.reshape(2, rows // 2, 2, cols // 2, 2).mean(axis=(2, 4))]
    ppermute x6 -> x0, waiting for transfers between devices: 10 us -> none  [the longest x3 9.99 us: padded_2(): after = lax.ppermute(first, axis, down)]
  transfers between devices with their start and end apart: 6 -> 0, of which waited for: 3 -> 0; matrix products, arithmetic and copies ran while one was open for 0% -> 0% of each run, Pallas kernels for 0% -> 0%
where the time goes in v1:
time: 24.5 us; the launch traced here: 24.1 us
  Pallas kernels  14.7 us (60%)
  local copies, waits for them, and re-layouts  8.77 us (36%)
  between operations  0.64 us (3%)
    pallas_call x1, Pallas kernels, body(): pl.pallas_call(kernel, out_shape=outs, in_specs=[anywhere] * 3 + [pl.Bloc...  14.7 us
    unnamed x6, local copies, waits for them, and re-layouts  8.77 us

profile of v1, /device:TPU:1, one launch (start us, length us, event | category | flops | bytes accessed | tf_op | source)
XLA Modules:
  0.0 24.1 jit_solution(6024357076639712393)
XLA Ops:
  0.6 14.7 %composite.1 = (s32[16,2048]{1,0:T(8,128)}, s32[16,2048]{1,0:T(8,128)}, s32[16,2048]{1,0:T(8,128)}, f32[2,8,1024]{2,1,0:T(8,128)}, f32[2,4,512]{2,1,0:T(4,128)}, /*index=5*/f32[2,2,256]{2,1,0:T(2,128)}) custom-call(s32[12,32,2048]{2,1,0:T(8,128)} %red.1, s32[12,32,2048]{2,1,0:T(8,128)} %nir.1, s32[12,32,2048]{2,1,0:T(8,128)} %cloud.1, s32[12]{0:T(128)} %ords.1), custom_call_target="tpu_custom_call" | custom-call | tf_op jit(solution)/shard_map/composite/pallas_call | solution.py:317
  15.4 1.6 %copy.16 = s32[16,2048]{1,0:T(8,128)} copy(s32[16,2048]{1,0:T(8,128)} %get-tuple-element.12) | data formatting | bytes 262144
  16.9 1.6 %copy.17 = s32[16,2048]{1,0:T(8,128)} copy(s32[16,2048]{1,0:T(8,128)} %get-tuple-element.13) | data formatting | bytes 262144
  18.5 1.6 %copy.18 = s32[16,2048]{1,0:T(8,128)} copy(s32[16,2048]{1,0:T(8,128)} %get-tuple-element.14) | data formatting | bytes 262144
  20.1 1.5 %copy.19 = f32[2,8,1024]{2,1,0:T(8,128)} copy(f32[2,8,1024]{2,1,0:T(8,128)} %get-tuple-element.15) | data formatting | bytes 131072
  21.5 1.3 %copy.20 = f32[2,4,512]{2,1,0:T(4,128)} copy(f32[2,4,512]{2,1,0:T(4,128)} %get-tuple-element.16) | data formatting | bytes 32768
  22.9 1.3 %copy.21 = f32[2,2,256]{2,1,0:T(2,128)} copy(f32[2,2,256]{2,1,0:T(2,128)} %get-tuple-element.17) | data formatting | bytes 8192

commit v2 on v1

--- a/solution.py
+++ b/solution.py
@@ -305,6 +305,16 @@
         to_outer.wait_send()
 
 
+def write_out(*refs):
+    count = len(refs) // 2
+    semaphores = refs[-1]
+    copies = [pltpu.make_async_copy(refs[n], refs[count + n], semaphores.at[n]) for n in range(count)]
+    for copy in copies:
+        copy.start()
+    for copy in copies:
+        copy.wait()
+
+
 def body(red_band, nir_band, cloud_class, date_ordinal):
     dates, strip, width = red_band.shape
     own = strip // 2
@@ -313,10 +323,11 @@
     anywhere = pl.BlockSpec(memory_space=pl.ANY)
     outs = [jax.ShapeDtypeStruct((own, width), jnp.int32)] * 3
     outs += [jax.ShapeDtypeStruct((2, own >> n, width >> n), jnp.float32) for n in range(1, LEVELS + 1)]
+    kept = [pltpu.VMEM(out.shape, out.dtype) for out in outs]
     stream = pltpu.VMEM((4, dates, chunk, width), jnp.int32)
-    return pl.pallas_call(
+    results = pl.pallas_call(
         kernel,
-        out_shape=outs,
+        out_shape=kept,
         in_specs=[anywhere] * 3 + [pl.BlockSpec(memory_space=pltpu.SMEM)],
         out_specs=[whole] * 6,
         scratch_shapes=[
@@ -337,6 +348,14 @@
         compiler_params=pltpu.CompilerParams(collective_id=0, has_side_effects=True),
         name="composite",
     )(red_band, nir_band, cloud_class, date_ordinal)
+    return pl.pallas_call(
+        write_out,
+        out_shape=outs,
+        in_specs=[whole] * 6,
+        out_specs=[anywhere] * 6,
+        scratch_shapes=[pltpu.SemaphoreType.DMA((6,))],
+        name="write_out",
+    )(*[pltpu.with_memory_space_constraint(result, pltpu.VMEM) for result in results])
 
 
 def solution(mesh):

time: 24.5 us -> 15.6 us (0.64)
  local copies, waits for them, and re-layouts: 8.77 us -> 0 us
    unnamed x6 -> x0, local copies, waits for them, and re-layouts: 8.77 us -> none
    pallas_call x1 -> x2, Pallas kernels: 14.7 us -> 14.8 us  [the longest x1 14 us: body(): pl.pallas_call(kernel, out_shape=kept, in_specs=[anywhere] * 3 + [pl.Bloc...]
where the time goes in v2:
time: 15.6 us; the launch traced here: 15.4 us
  Pallas kernels  14.8 us (95%)
  between operations  0.64 us (4%)
    pallas_call x1, Pallas kernels, body(): pl.pallas_call(kernel, out_shape=kept, in_specs=[anywhere] * 3 + [pl.Bloc...  14 us
    pallas_call x1, Pallas kernels, body(): pl.pallas_call(write_out, out_shape=outs, in_specs=[whole] * 6, out_specs...  0.82 us

profile of v2, /device:TPU:1, one launch (start us, length us, event | category | flops | bytes accessed | tf_op | source)
XLA Modules:
  0.0 15.4 jit_solution(10099063735571189228)
XLA Ops:
  0.6 14.0 %composite.1 = (s32[16,2048]{1,0:T(8,128)S(1)}, s32[16,2048]{1,0:T(8,128)S(1)}, s32[16,2048]{1,0:T(8,128)S(1)}, f32[2,8,1024]{2,1,0:T(8,128)S(1)}, f32[2,4,512]{2,1,0:T(4,128)S(1)}, /*index=5*/f32[2,2,256]{2,1,0:T(2,128)S(1)}) custom-call(s32[12,32,2048]{2,1,0:T(8,128)} %red.1, s32[12,32,2048]{2,1,0:T(8,128)} %nir.1, s32[12,32,2048]{2,1,0:T(8,128)} %cloud.1, ...), custom_call_target="tpu_custom_call" | custom-call | tf_op jit(solution)/shard_map/composite/pallas_call | solution.py:328
  14.6 0.8 %write_out.1 = (s32[16,2048]{1,0:T(8,128)}, s32[16,2048]{1,0:T(8,128)}, s32[16,2048]{1,0:T(8,128)}, f32[2,8,1024]{2,1,0:T(8,128)}, f32[2,4,512]{2,1,0:T(4,128)}, /*index=5*/f32[2,2,256]{2,1,0:T(2,128)}) custom-call(s32[16,2048]{1,0:T(8,128)S(1)} %get-tuple-element.12.refs_0_, s32[16,2048]{1,0:T(8,128)S(1)} %get-tuple-element.13.refs_1_, ...), custom_call_target="tpu_custom_call" | custom-call | tf_op jit(solution)/shard_map/write_out/pallas_call | solution.py:351

commit v3 on v2

--- a/solution.py
+++ b/solution.py
@@ -13,7 +13,8 @@
 FLAG = 1 << 30
 SCALE_BAND = 2.0**-30
 LANES = 128
-WIDTH = 256
+WIDTH = 512
+PARTS = 2
 MESH = pl.DeviceIdType.MESH
 
 
@@ -34,7 +35,7 @@
     low = n0a * r0b - n0b * r0a + ((ord_b - ord_a) >> 31)
     mid = (n1a * r0b + n0a * r1b) - (n1b * r0a + n0b * r1a) + (low >> LIMB_BITS)
     high = n1a * r1b - n1b * r1a + (mid >> LIMB_BITS)
-    return high + (clear_a - clear_b) >= 0
+    return high >= clear_b - clear_a
 
 
 def pick(take, first, second):
@@ -70,9 +71,9 @@
 
 
 def kernel(
-    red, nir, cloud, ords, out_red, out_nir, out_ord, out_1, out_2, out_3,
+    red, nir, cloud, ordinals, out_red, out_nir, out_ord, out_1, out_2, out_3,
     in_red, in_nir, in_cloud, best, arrived, wide_0, ybuf, wide_1, wide_2, zbuf,
-    load_sem, send_sem, recv_sem,
+    ords, load_sem, order_sem, send_sem, recv_sem,
 ):
     tile = lax.axis_index("tiles")
     strip_index = lax.axis_index("rows")
@@ -88,17 +89,24 @@
     rows_of = [(3 - 3 * core) * chunk, 3 * core * chunk, (2 - core) * chunk, (1 + core) * chunk]
 
     loads = []
+    piece = width // PARTS
     for slot, begin in enumerate(rows_of):
         begin = pl.multiple_of(begin, chunk)
-        group = [
-            pltpu.make_async_copy(
-                source.at[:, pl.ds(begin, chunk), :], target.at[slot], load_sem.at[slot, number]
-            )
-            for number, (source, target) in enumerate(((red, in_red), (nir, in_nir), (cloud, in_cloud)))
-        ]
-        for copy in group:
-            copy.start()
-        loads.append(group)
+        for part in range(PARTS):
+            columns = pl.ds(part * piece, piece)
+            group = [
+                pltpu.make_async_copy(
+                    source.at[:, pl.ds(begin, chunk), columns],
+                    target.at[slot, :, :, columns],
+                    load_sem.at[slot, part, number],
+                )
+                for number, (source, target) in enumerate(((red, in_red), (nir, in_nir), (cloud, in_cloud)))
+            ]
+            for copy in group:
+                copy.start()
+            loads.append(group)
+    order_copy = pltpu.make_async_copy(ordinals, ords, order_sem)
+    order_copy.start()
 
     barrier = pltpu.get_barrier_semaphore()
     pl.semaphore_signal(barrier, inc=1, device_id=partner, device_id_type=MESH)
@@ -113,7 +121,7 @@
 
     @pl.when(jnp.logical_not(has_outer))
     def _():
-        ybuf[3] = jnp.zeros(ybuf.shape[1:], jnp.float32)
+        ybuf[2] = jnp.zeros(ybuf.shape[1:], jnp.float32)
         zbuf[2] = jnp.zeros(zbuf.shape[1:], jnp.float32)
 
     for wide in (wide_0, wide_1, wide_2):
@@ -121,12 +129,14 @@
         wide[:, 0:LANES] = edge
         wide[:, wide.shape[1] - LANES :] = edge
 
-    def find_best(slot):
-        for copy in loads[slot]:
+    order_copy.wait()
+
+    def find_best(slot, part):
+        for copy in loads[slot * PARTS + part]:
             copy.wait()
 
         def step(number, unused):
-            columns = pl.ds(pl.multiple_of(number * WIDTH, WIDTH), WIDTH)
+            columns = pl.ds(pl.multiple_of(number * WIDTH + part * piece, WIDTH), WIDTH)
 
             def entry(date):
                 red_hi, red_lo = limbs(in_red[slot, date, :, columns])
@@ -144,19 +154,26 @@
             best[slot, 2, :, columns] = clear + order
             return unused
 
-        lax.fori_loop(0, width // WIDTH, step, 0)
-
-    def send_best(slot, place):
+        lax.fori_loop(0, piece // WIDTH, step, 0)
+
+    partner_sends = []
+
+    def send_best(slot, place, part):
+        columns = pl.ds(part * piece, piece)
         copy = pltpu.make_async_remote_copy(
-            src_ref=best.at[slot],
-            dst_ref=arrived.at[place],
-            send_sem=send_sem.at[place],
-            recv_sem=recv_sem.at[place],
+            src_ref=best.at[slot, :, :, columns],
+            dst_ref=arrived.at[place, :, :, columns],
+            send_sem=send_sem.at[3 + place * PARTS + part],
+            recv_sem=recv_sem.at[3 + place * PARTS + part],
             device_id=partner,
             device_id_type=MESH,
         )
         copy.start()
-        return copy
+        partner_sends.append(copy)
+
+    def wait_best(place):
+        for copy in partner_sends[place * PARTS : (place + 1) * PARTS]:
+            copy.wait_recv()
 
     def merge(slot, place, out_row):
         def step(number, unused):
@@ -187,18 +204,21 @@
         for number, block in enumerate(filter_columns(wide_0, column_weights)):
             ybuf[place, :, number * LANES : (number + 1) * LANES] = block
 
-    find_best(0)
-    pl.semaphore_wait(barrier, 1 + has_outer.astype(jnp.int32))
-    send_0 = send_best(0, 0)
-    find_best(1)
-    send_0.wait_recv()
+    for part in range(PARTS):
+        find_best(0, part)
+        if part == 0:
+            pl.semaphore_wait(barrier, 1 + has_outer.astype(jnp.int32))
+        send_best(0, 0, part)
+    for part in range(PARTS):
+        find_best(1, part)
+    wait_best(0)
     merge(1, 0, core * chunk)
     columns_of(0)
     halo = pltpu.make_async_remote_copy(
         src_ref=ybuf.at[0],
-        dst_ref=ybuf.at[3],
-        send_sem=send_sem.at[3],
-        recv_sem=recv_sem.at[3],
+        dst_ref=ybuf.at[2],
+        send_sem=send_sem.at[0],
+        recv_sem=recv_sem.at[0],
         device_id=outer,
         device_id_type=MESH,
     )
@@ -207,29 +227,32 @@
     def _():
         halo.start()
 
-    find_best(2)
-    send_1 = send_best(2, 1)
-    find_best(3)
-    send_2 = send_best(3, 2)
-    send_1.wait_recv()
+    for slot, place in ((2, 1), (3, 2)):
+        for part in range(PARTS):
+            find_best(slot, part)
+            send_best(slot, place, part)
+    wait_best(1)
     merge(3, 1, (1 - core) * chunk)
     columns_of(1)
 
     quarter = chunk // 2
-    m = iota((4 * chunk, 8 * chunk), 0)
-    band_m = m // (2 * chunk)
-    within = m % (2 * chunk)
-    row_1 = jnp.where(within < chunk, within, jnp.where(within < chunk + quarter, within - chunk - quarter, within - quarter))
-    c = iota((4 * chunk, 8 * chunk), 1)
-    place = c // (2 * chunk)
-    band_c = (c // chunk) % 2
-    from_core_0 = jnp.where(place == 3, -chunk, place * chunk)
-    from_core_1 = chunk - from_core_0
-    row_0 = jnp.where(core == 0, from_core_0, from_core_1) + c % chunk
-    from_edge = jnp.where(core == 0, row_1, chunk - 1 - row_1)
-    inside = from_edge >= jnp.where(has_outer, -chunk, 0)
-    rows_1 = jnp.where((band_m == band_c) & inside, taps(row_0 - (2 * row_1 - 2)), 0.0)
-    rows_1 = rows_1.astype(jnp.bfloat16)
+    def row_weights(first, count):
+        shape = (4 * chunk, count * 2 * chunk)
+        m = iota(shape, 0)
+        band_m = m // (2 * chunk)
+        within = m % (2 * chunk)
+        row_1 = jnp.where(within < chunk, within, jnp.where(within < chunk + quarter, within - chunk - quarter, within - quarter))
+        c = iota(shape, 1)
+        place = c // (2 * chunk) + first
+        band_c = (c // chunk) % 2
+        from_core_0 = jnp.where(place == 2, -chunk, jnp.where(place == 3, 2 * chunk, place * chunk))
+        from_core_1 = chunk - from_core_0
+        row_0 = jnp.where(core == 0, from_core_0, from_core_1) + c % chunk
+        from_edge = jnp.where(core == 0, row_1, chunk - 1 - row_1)
+        inside = from_edge >= jnp.where(has_outer, -chunk, 0)
+        return jnp.where((band_m == band_c) & inside, taps(row_0 - (2 * row_1 - 2)), 0.0).astype(jnp.bfloat16)
+
+    rows_1a, rows_1b = row_weights(0, 3), row_weights(3, 1)
 
     m = iota((3 * chunk, 4 * chunk), 0)
     packed = m >= 2 * chunk
@@ -250,53 +273,57 @@
     rows_3 = jnp.where(m // chunk == (c % chunk) // quarter, taps(row_2 - (2 * (m % chunk) - 2)), 0.0)
     rows_3 = rows_3.astype(jnp.bfloat16)
 
-    send_2.wait_recv()
-    merge(2, 2, None)
-    columns_of(2)
-
-    @pl.when(has_outer)
-    def _():
-        halo.wait_recv()
-
-    level_1 = dot_split(rows_1, ybuf[...].reshape(8 * chunk, half), True)
-    wide_1[:, LANES : LANES + half] = level_1
-    out_1[0] = level_1[0:chunk]
-    out_1[1] = level_1[2 * chunk : 3 * chunk]
-    data = jnp.concatenate(filter_columns(wide_1, column_weights), axis=1)
-    level_2 = dot_split(rows_2, data, True)
-    wide_2[:, LANES : LANES + half // 2] = level_2[2 * chunk :]
-    out_2[0] = level_2[0:quarter]
-    out_2[1] = level_2[chunk : chunk + quarter]
-    zbuf[0] = jnp.concatenate(filter_columns(wide_2, column_weights), axis=1)
-
-    def send_z(slot, device):
+    def next_levels(level_1):
+        wide_1[:, LANES : LANES + half] = level_1
+        data = jnp.concatenate(filter_columns(wide_1, column_weights), axis=1)
+        level_2 = dot_split(rows_2, data, True)
+        wide_2[:, LANES : LANES + half // 2] = level_2[2 * chunk :]
+        return level_2, jnp.concatenate(filter_columns(wide_2, column_weights), axis=1)
+
+    def send_z(source, slot, device):
         return pltpu.make_async_remote_copy(
-            src_ref=zbuf.at[0],
+            src_ref=zbuf.at[source],
             dst_ref=zbuf.at[slot],
-            send_sem=send_sem.at[3 + slot],
-            recv_sem=recv_sem.at[3 + slot],
+            send_sem=send_sem.at[slot],
+            recv_sem=recv_sem.at[slot],
             device_id=device,
             device_id_type=MESH,
         )
 
-    to_partner, to_outer = send_z(1, partner), send_z(2, outer)
+    to_partner, to_outer = send_z(0, 1, partner), send_z(3, 2, outer)
+
+    @pl.when(has_outer)
+    def _():
+        halo.wait_recv()
+
+    level_1a = dot_split(rows_1a, ybuf[0:3].reshape(6 * chunk, half), True)
+    zbuf[3] = next_levels(level_1a)[1]
 
     @pl.when(has_outer)
     def _():
         to_outer.start()
 
+    wait_best(2)
+    merge(2, 2, None)
+    columns_of(3)
+    level_1 = level_1a + dot_split(rows_1b, ybuf[3], True)
+    level_2, zbuf[0] = next_levels(level_1)
     to_partner.start()
+    out_1[0] = level_1[0:chunk]
+    out_1[1] = level_1[2 * chunk : 3 * chunk]
+    out_2[0] = level_2[0:quarter]
+    out_2[1] = level_2[chunk : chunk + quarter]
     to_partner.wait_recv()
 
     @pl.when(has_outer)
     def _():
         to_outer.wait_recv()
 
-    level_3 = dot_split(rows_3, zbuf[...].reshape(3 * chunk, zbuf.shape[2]), True)
+    level_3 = dot_split(rows_3, zbuf[0:3].reshape(3 * chunk, zbuf.shape[2]), True)
     out_3[0] = level_3[0 : quarter // 2]
     out_3[1] = level_3[chunk : chunk + quarter // 2]
 
-    for copy in (send_0, send_1, send_2, to_partner):
+    for copy in partner_sends + [to_partner]:
         copy.wait_send()
 
     @pl.when(has_outer)
@@ -328,7 +355,7 @@
     results = pl.pallas_call(
         kernel,
         out_shape=kept,
-        in_specs=[anywhere] * 3 + [pl.BlockSpec(memory_space=pltpu.SMEM)],
+        in_specs=[anywhere] * 4,
         out_specs=[whole] * 6,
         scratch_shapes=[
             stream,
@@ -340,10 +367,12 @@
             pltpu.VMEM((4, 2 * chunk, width // 2), jnp.float32),
             pltpu.VMEM((4 * chunk, width // 2 + 2 * LANES), jnp.float32),
             pltpu.VMEM((chunk, width // 4 + 2 * LANES), jnp.float32),
-            pltpu.VMEM((3, chunk, width // 8), jnp.float32),
-            pltpu.SemaphoreType.DMA((4, 3)),
-            pltpu.SemaphoreType.DMA((6,)),
-            pltpu.SemaphoreType.DMA((6,)),
+            pltpu.VMEM((4, chunk, width // 8), jnp.float32),
+            pltpu.SMEM((dates,), jnp.int32),
+            pltpu.SemaphoreType.DMA((4, PARTS, 3)),
+            pltpu.SemaphoreType.DMA,
+            pltpu.SemaphoreType.DMA((3 + 3 * PARTS,)),
+            pltpu.SemaphoreType.DMA((3 + 3 * PARTS,)),
         ],
         compiler_params=pltpu.CompilerParams(collective_id=0, has_side_effects=True),
         name="composite",

time: 15.6 us -> 13 us (0.83)
  the two profiles are of different devices: /device:TPU:1 before, /device:TPU:0 now
where the time goes in v3:
time: 13 us; the launch traced here: 12.9 us
  Pallas kernels  12.2 us (94%)
  between operations  0.64 us (5%)
    pallas_call x1, Pallas kernels, body(): pl.pallas_call(kernel, out_shape=kept, in_specs=[anywhere] * 4, out_specs...  11.4 us
    pallas_call x1, Pallas kernels, body(): pl.pallas_call(write_out, out_shape=outs, in_specs=[whole] * 6, out_specs...  0.82 us

profile of v3, /device:TPU:0, one launch (start us, length us, event | category | flops | bytes accessed | tf_op | source)
XLA Modules:
  0.0 12.9 jit_solution(8494537754070811231)
XLA Ops:
  0.6 11.4 %composite.1 = (s32[16,2048]{1,0:T(8,128)S(1)}, s32[16,2048]{1,0:T(8,128)S(1)}, s32[16,2048]{1,0:T(8,128)S(1)}, f32[2,8,1024]{2,1,0:T(8,128)S(1)}, f32[2,4,512]{2,1,0:T(4,128)S(1)}, /*index=5*/f32[2,2,256]{2,1,0:T(2,128)S(1)}) custom-call(s32[12,32,2048]{2,1,0:T(8,128)} %red.1, s32[12,32,2048]{2,1,0:T(8,128)} %nir.1, s32[12,32,2048]{2,1,0:T(8,128)} %cloud.1, ...), custom_call_target="tpu_custom_call" | custom-call | tf_op jit(solution)/shard_map/composite/pallas_call | solution.py:355
  12.1 0.8 %write_out.1 = (s32[16,2048]{1,0:T(8,128)}, s32[16,2048]{1,0:T(8,128)}, s32[16,2048]{1,0:T(8,128)}, f32[2,8,1024]{2,1,0:T(8,128)}, f32[2,4,512]{2,1,0:T(4,128)}, /*index=5*/f32[2,2,256]{2,1,0:T(2,128)}) custom-call(s32[16,2048]{1,0:T(8,128)S(1)} %get-tuple-element.12.refs_0_, s32[16,2048]{1,0:T(8,128)S(1)} %get-tuple-element.13.refs_1_, ...), custom_call_target="tpu_custom_call" | custom-call | tf_op jit(solution)/shard_map/write_out/pallas_call | solution.py:380

commit v4 on v3

--- a/solution.py
+++ b/solution.py
@@ -142,12 +142,15 @@
                 red_hi, red_lo = limbs(in_red[slot, date, :, columns])
                 nir_hi, nir_lo = limbs(in_nir[slot, date, :, columns])
                 clear = jnp.where(in_cloud[slot, date, :, columns] == 0, FLAG, 0)
-                return (red_hi, red_lo, nir_hi, nir_lo, clear, jnp.full((chunk, WIDTH), ords[date], jnp.int32))
-
-            current = entry(0)
-            for date in range(1, dates):
+                return (red_hi, red_lo, nir_hi, nir_lo, clear, ords[date])
+
+            current = None
+            for date in range(0, dates, 2):
                 other = entry(date)
-                current = pick(take_first(other, current), other, current)
+                if date + 1 < dates:
+                    later = entry(date + 1)
+                    other = pick(take_first(later, other), later, other)
+                current = other if current is None else pick(take_first(other, current), other, current)
             value_red, value_nir, clear, order = joined(current)
             best[slot, 0, :, columns] = value_red
             best[slot, 1, :, columns] = value_nir

time: 13 us -> 12.8 us (0.985)
  Pallas kernels: 12.2 us -> 12 us
    pallas_call x1, Pallas kernels: 11.4 us -> 11.2 us  [body(): pl.pallas_call(kernel, out_shape=kept, in_specs=[anywhere] * 4, out_specs...]
where the time goes in v4:
time: 12.8 us; the launch traced here: 12.6 us
  Pallas kernels  12 us (94%)
  between operations  0.64 us (5%)
    pallas_call x1, Pallas kernels, body(): pl.pallas_call(kernel, out_shape=kept, in_specs=[anywhere] * 4, out_specs...  11.2 us
    pallas_call x1, Pallas kernels, body(): pl.pallas_call(write_out, out_shape=outs, in_specs=[whole] * 6, out_specs...  0.82 us

profile of v4, /device:TPU:0, one launch (start us, length us, event | category | flops | bytes accessed | tf_op | source)
XLA Modules:
  0.0 12.6 jit_solution(5453223259059947568)
XLA Ops:
  0.6 11.2 %composite.1 = (s32[16,2048]{1,0:T(8,128)S(1)}, s32[16,2048]{1,0:T(8,128)S(1)}, s32[16,2048]{1,0:T(8,128)S(1)}, f32[2,8,1024]{2,1,0:T(8,128)S(1)}, f32[2,4,512]{2,1,0:T(4,128)S(1)}, /*index=5*/f32[2,2,256]{2,1,0:T(2,128)S(1)}) custom-call(s32[12,32,2048]{2,1,0:T(8,128)} %red.1, s32[12,32,2048]{2,1,0:T(8,128)} %nir.1, s32[12,32,2048]{2,1,0:T(8,128)} %cloud.1, ...), custom_call_target="tpu_custom_call" | custom-call | tf_op jit(solution)/shard_map/composite/pallas_call | solution.py:358
  11.8 0.8 %write_out.1 = (s32[16,2048]{1,0:T(8,128)}, s32[16,2048]{1,0:T(8,128)}, s32[16,2048]{1,0:T(8,128)}, f32[2,8,1024]{2,1,0:T(8,128)}, f32[2,4,512]{2,1,0:T(4,128)}, /*index=5*/f32[2,2,256]{2,1,0:T(2,128)}) custom-call(s32[16,2048]{1,0:T(8,128)S(1)} %get-tuple-element.12.refs_0_, s32[16,2048]{1,0:T(8,128)S(1)} %get-tuple-element.13.refs_1_, ...), custom_call_target="tpu_custom_call" | custom-call | tf_op jit(solution)/shard_map/write_out/pallas_call | solution.py:383
